TPU v7x, 256 devices: a whole 4x4x8 slice. The times are simulated.
256 devices in a mesh: seq: 4 (over x_hi, core), ctx: 8 (over z), head: 8 (over x_lo, y).
Axes of the slice: x: 4 (x_hi: 2, x_lo: 2; x = x_hi * 2 + x_lo), y: 4, z: 8, core: 2. Of those that a mesh axis runs over, the one named last changes fastest.
Arguments:
- stream: bfloat16 [4, 512, 2880], P('seq', 'ctx'), may hold values from -6 to 6
- query_weight: bfloat16 [2880, 4096], P(None, 'head'), may hold values from -0.109375 to 0.109375
- cache_keys: bfloat16 [4, 16384, 8, 64], P('seq', 'ctx', 'head'), may hold values from -1000 to 1000
- cache_values: bfloat16 [4, 16384, 8, 64], P('seq', 'ctx', 'head'), may hold values from -6 to 6
- new_keys: bfloat16 [4, 512, 8, 64], P('seq', 'ctx', 'head'), may hold values from -18 to 18
- new_values: bfloat16 [4, 512, 8, 64], P('seq', 'ctx', 'head'), may hold values from -6 to 6
- out_weight: bfloat16 [4096, 2880], P('head'), may hold values from -0.09375 to 0.09375
- norm_gain: float32 [2880], replicated, may hold values from 0.5 to 1.5
- expert_ids: int32 [4, 512, 4], P('seq', 'ctx'), may hold values from 0 to 31, all different within a row; in each aligned block of 64 rows (0 to 63, 64 to 127, ..., all dimensions but the last counted through in order) at most 16 rows name the same one
- expert_weights: float32 [4, 512, 4], P('seq', 'ctx'), may hold values from 0.1 to 1
- gate_weight: bfloat16 [32, 2880, 2880], P(('seq', 'ctx'), None, 'head'), may hold values from -0.109375 to 0.109375
- up_weight: bfloat16 [32, 2880, 2880], P(('seq', 'ctx'), None, 'head'), may hold values from -0.109375 to 0.109375
- down_weight: bfloat16 [32, 2880, 2880], P(('seq', 'ctx'), 'head'), may hold values from -0.109375 to 0.109375
Outputs:
- mixed: bfloat16 [4, 512, 2880], P('seq', 'ctx', 'head')
Inputs may be any that keep to these rules, and one draw needn't show every extreme that they name: `expert_ids`: in each aligned block of 64 rows (the tokens of one device) no expert is named by more than 16 rows; each row names 4 different experts.
All inputs are finite; a program needn't handle non-finite values.
Results may differ from a plain program's by a relative error of at most 0.015.
Values may be sent and summed in bfloat16 or wider, within the bound.
A program may use at most 64 MiB of HBM per device.

v0:
```python
import math
import jax
import jax.numpy as jnp
from jax import lax
from jax.sharding import PartitionSpec as P

CAP = 16


def sent_to_all(array, axis):
    copies = jnp.broadcast_to(array, (lax.axis_size(axis), *array.shape))
    return lax.all_to_all(copies, axis, split_axis=0, concat_axis=0, tiled=True)


def joined_along(tiles, dim):
    shape = list(tiles.shape[1:])
    shape[dim] *= tiles.shape[0]
    return jnp.moveaxis(tiles, 0, dim).reshape(shape)


def gathered_copies(array, axis, dim):
    tiles = sent_to_all(array, axis)
    return joined_along(tiles, dim)


def split_up(array, dim, count):
    before, after = (array.shape[:dim], array.shape[dim + 1 :])
    return jnp.moveaxis(array.reshape(*before, count, -1, *after), dim, 0)


def sent_and_summed(array, axis, dim):
    tiles = split_up(array, dim, lax.axis_size(axis))
    arrived = lax.all_to_all(tiles, axis, split_axis=0, concat_axis=0, tiled=True)
    return arrived.astype(jnp.float32).sum(axis=0)


def taken_together(array, axis):
    return sent_to_all(array, axis).sum(axis=0)


def body(
    stream,
    query_weight,
    cache_keys,
    cache_values,
    new_keys,
    new_values,
    out_weight,
    norm_gain,
    expert_ids,
    expert_weights,
    gate_weight,
    up_weight,
    down_weight,
):
    tokens = stream[0]
    count = tokens.shape[0]
    model = tokens.shape[1]
    kv_local = cache_keys.shape[2]
    head_dim = cache_keys.shape[3]
    group = query_weight.shape[1] // (kv_local * head_dim)
    cache_len = cache_keys.shape[1]
    height = count * group
    cycles = lax.axis_size("ctx")
    place = lax.axis_index("ctx")
    scale = 1.0 / math.sqrt(head_dim)
    query = jnp.dot(tokens, query_weight, preferred_element_type=jnp.float32).astype(jnp.bfloat16)
    query = (
        query.reshape(count, kv_local, group, head_dim)
        .transpose(1, 0, 2, 3)
        .reshape(kv_local, height, head_dim)
    )
    keys = jnp.concatenate([cache_keys[0], new_keys[0]], axis=0).transpose(1, 0, 2)
    values = jnp.concatenate([cache_values[0], new_values[0]], axis=0).transpose(1, 0, 2)
    extent = keys.shape[1]
    key_index = lax.broadcasted_iota(jnp.int32, (height, extent), 1)
    tok_index = lax.broadcasted_iota(jnp.int32, (height, extent), 0) // group
    fresh = key_index - cache_len
    blank = (
        jnp.full((kv_local, height), -jnp.inf, jnp.float32),
        jnp.zeros((kv_local, height), jnp.float32),
        jnp.zeros((kv_local, height, head_dim), jnp.float32),
    )

    def absorb(block, state, sources):
        top, total, numerator = state
        anchor = sources[:, None]
        allowed = (
            (key_index < cache_len) | (place < anchor) | (place == anchor) & (fresh <= tok_index)
        )
        scores = jnp.einsum("hrd,hkd->hrk", block, keys, preferred_element_type=jnp.float32) * scale
        scores = jnp.where(allowed[None], scores, -jnp.inf)
        new_top = jnp.max(scores, axis=-1)
        weights = jnp.exp(scores - new_top[..., None])
        fade = jnp.exp(top - new_top)
        total = total * fade + jnp.sum(weights, axis=-1)
        numerator = numerator * fade[..., None] + jnp.einsum(
            "hrk,hkd->hrd", weights.astype(jnp.bfloat16), values, preferred_element_type=jnp.float32
        )
        return (new_top, total, numerator)

    everyone = gathered_copies(query[None], "ctx", 0)

    def partial_state(operands):
        block, source = operands
        return absorb(block, blank, jnp.full((height,), source, jnp.int32))

    pieces = lax.map(partial_state, (everyone, lax.iota(jnp.int32, cycles)))
    tops, totals, numerators = lax.all_to_all(
        pieces, "ctx", split_axis=0, concat_axis=0, tiled=True
    )
    top = jnp.max(tops, axis=0)
    fade = jnp.exp(tops - top[None])
    total = jnp.sum(totals * fade, axis=0)
    numerator = jnp.sum(numerators * fade[..., None], axis=0)
    attn = (numerator / total[..., None]).astype(jnp.bfloat16)
    attn = (
        attn.reshape(kv_local, count, group, head_dim)
        .transpose(1, 0, 2, 3)
        .reshape(count, kv_local * group * head_dim)
    )
    projected = jnp.dot(attn, out_weight, preferred_element_type=jnp.float32)
    width = model // lax.axis_size("head")
    offset = lax.axis_index("head") * width
    resid_own = lax.dynamic_slice_in_dim(tokens, offset, width, 1).astype(
        jnp.float32
    ) + sent_and_summed(projected.astype(jnp.bfloat16), "head", 1)
    power = taken_together(jnp.sum(resid_own * resid_own, axis=-1), "head")
    gain_own = lax.dynamic_slice_in_dim(norm_gain, offset, width, 0)
    normed = (resid_own * lax.rsqrt(power[:, None] / model + 1e-05) * gain_own).astype(jnp.bfloat16)
    experts = lax.axis_size("seq") * lax.axis_size("ctx")
    slots = experts * CAP
    chosen = expert_ids[0].reshape(-1)
    onehot = (chosen[:, None] == lax.broadcasted_iota(jnp.int32, (1, experts), 1)).astype(jnp.int32)
    before = jnp.cumsum(onehot, axis=0) - onehot
    target = chosen * CAP + jnp.sum(before * onehot, axis=1)
    matches = target[None, :] == lax.broadcasted_iota(jnp.int32, (slots, 1), 0)
    select = jnp.sum(matches.astype(jnp.float32).reshape(slots, count, -1), axis=-1).astype(
        jnp.bfloat16
    )
    packed = jnp.dot(select, normed, preferred_element_type=jnp.float32).astype(jnp.bfloat16)
    packed = packed.reshape(experts, CAP, normed.shape[1])
    arrived = lax.all_to_all(packed, ("seq", "ctx"), split_axis=0, concat_axis=0, tiled=True)
    rows = arrived.reshape(slots, normed.shape[1])
    piece = lax.all_gather(rows, "head", axis=1, tiled=True)
    gate_rows = gate_weight[0]
    up_rows = up_weight[0]
    gate = jnp.dot(piece, gate_rows, preferred_element_type=jnp.float32)
    up = jnp.dot(piece, up_rows, preferred_element_type=jnp.float32)
    hidden = (gate * jax.nn.sigmoid(1.702 * gate) * (up + 1.0)).astype(jnp.bfloat16)
    columns = down_weight[0]
    expert_out = sent_and_summed(
        jnp.einsum("fd,rf->dr", columns, hidden, preferred_element_type=jnp.float32).astype(
            jnp.bfloat16
        ),
        "head",
        0,
    ).astype(jnp.bfloat16)
    returned = lax.all_to_all(expert_out, ("seq", "ctx"), split_axis=1, concat_axis=1, tiled=True)
    spread_weights = jnp.where(matches.T, expert_weights[0].reshape(-1)[:, None], 0.0)
    spread_weights = jnp.sum(spread_weights.reshape(count, -1, slots), axis=1)
    moe = lax.dot_general(
        spread_weights,
        returned.astype(jnp.float32),
        (((1,), (1,)), ((), ())),
        precision=lax.Precision.HIGHEST,
    )
    return (resid_own + moe).astype(jnp.bfloat16)[None]


def solution(mesh):
    in_specs = (
        P("seq", "ctx", None),
        P(None, "head"),
        P("seq", "ctx", "head", None),
        P("seq", "ctx", "head", None),
        P("seq", "ctx", "head", None),
        P("seq", "ctx", "head", None),
        P("head", None),
        P(),
        P("seq", "ctx", None),
        P("seq", "ctx", None),
        P(("seq", "ctx"), None, "head"),
        P(("seq", "ctx"), None, "head"),
        P(("seq", "ctx"), "head", None),
    )
    out_specs = P("seq", "ctx", "head")
    return jax.shard_map(body, mesh=mesh, in_specs=in_specs, out_specs=out_specs, check_vma=False)
```

profile of v0, /device:TPU:1, one launch (start us, length us, event | category | flops | bytes accessed | tf_op | source)
XLA Modules:
  0.0 326.2 jit_solution(1258331897230026775)
XLA Ops:
  6.5 2.7 convolution_convert_fusion.3
  10.4 9.0 %all-to-all-start = ((bf16[8,1,1,512,64]{3,4,2,1,0:T(8,128)(2,1)}), bf16[8,1,1,512,64]{3,4,2,1,0:T(8,128)(2,1)}, u32[]{:S(2)}, u32[]{:S(2)}) async-start(bf16[8,1,1,512,64]{3,4,2,1,0:T(8,128)(2,1)} %broadcast_in_dim.65), calls=%async_computation | async-start | bytes 1048576 | tf_op jit(solution)/shard_map/all_to_all | solution.py:12
  19.4 1.0 copy.57
  20.4 1.9 copy.58
  24.1 2.2 maximum_bitcast_fusion
  26.4 11.1 %all-to-all-done = bf16[8,1,1,512,64]{3,4,2,1,0:T(8,128)(2,1)} async-done(((bf16[8,1,1,512,64]{3,4,2,1,0:T(8,128)(2,1)}), bf16[8,1,1,512,64]{3,4,2,1,0:T(8,128)(2,1)}, u32[]{:S(2)}, u32[]{:S(2)}) %all-to-all-start) | async-done | bytes 524320 | tf_op jit(solution)/shard_map/all_to_all | solution.py:12
  37.4 55.5 %while.17 = (s32[]{:T(128)}, f32[8,1,512]{2,1,0:T(1,128)S(1)}, f32[8,1,512]{2,1,0:T(1,128)S(1)}, f32[8,1,512,64]{2,3,1,0:T(8,128)}, s32[8]{0:T(128)S(1)}, /*inde...) while((s32[]{:T(128)}, f32[8,1,512]{2,1,0:T(1,128)S(1)}, ...), condition=%wide.region_3.4_spmd.clone, body=%wide.region_0.3_spmd.clone.sunk | while | flops 290915840 | bytes 14024361 | solution.py:108
  39.3 3.0 fusion.82
  42.3 1.4 fusion.84
  46.2 3.0 fusion.82
  49.2 1.4 fusion.84
  53.1 3.0 fusion.82
  56.1 1.4 fusion.84
  60.1 3.0 fusion.82
  63.1 1.4 fusion.84
  67.0 3.0 fusion.82
  70.0 1.4 fusion.84
  73.9 3.0 fusion.82
  77.0 1.4 fusion.84
  80.9 3.0 fusion.82
  83.9 1.4 fusion.84
  87.8 3.0 fusion.82
  90.8 1.4 fusion.84
  92.9 9.0 %all_to_all.53 = f32[8,1,512]{2,1,0:T(1,128)S(1)} all-to-all(f32[8,1,512]{2,1,0:T(1,128)S(1)} %get-tuple-element.143), channel_id=1, replica_groups=mesh['seq'=4,'ctx'=8,'head'=8] {'ctx'}, dimensions={0} | all-to-all | bytes 32768 | tf_op jit(solution)/shard_map/all_to_all | solution.py:109
  102.0 9.0 %all_to_all.54 = f32[8,1,512]{2,1,0:T(1,128)S(1)} all-to-all(f32[8,1,512]{2,1,0:T(1,128)S(1)} %get-tuple-element.144), channel_id=1, replica_groups=mesh['seq'=4,'ctx'=8,'head'=8] {'ctx'}, dimensions={0} | all-to-all | bytes 32768 | tf_op jit(solution)/shard_map/all_to_all | solution.py:109
  110.9 4.2 %all-to-all-start.1 = ((f32[8,1,512,64]{2,3,1,0:T(8,128)}), f32[8,1,512,64]{2,3,1,0:T(8,128)}, u32[]{:S(2)}, u32[]{:S(2)}) async-start(f32[8,1,512,64]{2,3,1,0:T(8,128)} %get-tuple-element.142), calls=%async_computation.1 | async-start | bytes 2097152 | tf_op jit(solution)/shard_map/all_to_all | solution.py:109
  117.8 24.6 %all-to-all-done.1 = f32[8,1,512,64]{2,3,1,0:T(8,128)} async-done(((f32[8,1,512,64]{2,3,1,0:T(8,128)}), f32[8,1,512,64]{2,3,1,0:T(8,128)}, u32[]{:S(2)}, u32[]{:S(2)}) %all-to-all-start.1) | async-done | bytes 1048608 | tf_op jit(solution)/shard_map/all_to_all | solution.py:109
  142.4 1.4 multiply_reduce_fusion
  144.1 1.7 convolution_convert_fusion.1
  145.8 1.5 reshape.190
  148.1 5.1 %all-to-all-start.4 = ((bf16[8,64,360]{2,1,0:T(8,128)(2,1)}), bf16[8,64,360]{2,1,0:T(8,128)(2,1)S(1)}, u32[]{:S(2)}, u32[]{:S(2)}) async-start(bf16[8,64,360]{2,1,0:T(8,128)(2,1)} %bitcast.105), calls=%async_computation.4 | async-start | bytes 786432 | tf_op jit(solution)/shard_map/all_to_all | solution.py:33
  153.6 6.3 %all-to-all-done.4 = bf16[8,64,360]{2,1,0:T(8,128)(2,1)S(1)} async-done(((bf16[8,64,360]{2,1,0:T(8,128)(2,1)}), bf16[8,64,360]{2,1,0:T(8,128)(2,1)S(1)}, u32[]{:S(2)}, u32[]{:S(2)}) %all-to-all-start.4) | async-done | bytes 368672 | tf_op jit(solution)/shard_map/all_to_all | solution.py:33
  159.9 1.0 multiply_reduce_fusion.1
  161.6 3.3 %all-to-all-start.5 = ((f32[8,1,64]{2,1,0:T(1,128)}), f32[8,1,64]{2,1,0:T(1,128)S(1)}, u32[]{:S(2)}, u32[]{:S(2)}) async-start(f32[8,1,64]{2,1,0:T(1,128)} %broadcast_in_dim.69), calls=%async_computation.5 | async-start | bytes 8192 | tf_op jit(solution)/shard_map/all_to_all | solution.py:12
  165.8 3.9 %all-to-all-done.5 = f32[8,1,64]{2,1,0:T(1,128)S(1)} async-done(((f32[8,1,64]{2,1,0:T(1,128)}), f32[8,1,64]{2,1,0:T(1,128)S(1)}, u32[]{:S(2)}, u32[]{:S(2)}) %all-to-all-start.5) | async-done | bytes 2080 | tf_op jit(solution)/shard_map/all_to_all | solution.py:12
  169.8 2.0 convolution_convert_fusion.2
  171.8 1.2 copy.69
  173.0 23.9 %all_to_all.55 = bf16[32,16,360]{2,1,0:T(8,128)(2,1)} all-to-all(bf16[32,16,360]{2,1,0:T(8,128)(2,1)S(1)} %bitcast.126), channel_id=1, replica_groups=mesh['seq'=4,'ctx'=8,'head'=8] {'seq','ctx'}, dimensions={0} | all-to-all | bytes 737280 | tf_op jit(solution)/shard_map/all_to_all | solution.py:143
  196.9 1.9 copy.70
  198.8 36.6 %all-gather.2.cloned.1.call-done = bf16[512,2880]{0,1:T(8,128)(2,1)} async-done(((bf16[512,360]{0,1:T(8,128)(2,1)}), bf16[512,2880]{0,1:T(8,128)(2,1)}) %all-gather.2.cloned.1.call-update) | async-done | bytes 2949136 | tf_op jit(solution)/shard_map/all_gather | solution.py:145
  235.5 4.7 %fusion.30 = f32[512,360]{0,1:T(8,128)} fusion(bf16[512,2880]{0,1:T(8,128)(2,1)} %all-gather.2.cloned.1.call-done, bf16[1,2880,360]{1,2,0:T(8,128)(2,1)} %param.25), kind=kOutput, calls=%fused_computation.30 | convolution fusion | flops 1061683200 | bytes 5760000 | tf_op jit(solution)/shard_map/dot_general | solution.py:148
  240.1 7.9 %convolution_convert_fusion = bf16[512,2880]{0,1:T(8,128)(2,1)} fusion(bf16[1,360,2880]{2,1,0:T(8,128)(2,1)} %param.27, bf16[512,2880]{0,1:T(8,128)(2,1)} %all-gather.2.cloned.1.call-done, bf16[1,2880,360]{1,2,0:T(8,128)(2,1)} %param.26, f32[512,360]{0,1:T(8,128)} %fusion.30), kind=kOutput, calls=%fused_computation.25 | convolution fusion | flops 2126315520 | bytes 10782720 | tf_op jit(solution)/shard_map/fd,rf->dr/dot_general | solution.py:153
  248.1 37.1 %all_to_all.56 = bf16[8,360,512]{2,1,0:T(8,128)(2,1)} all-to-all(bf16[8,360,512]{2,1,0:T(8,128)(2,1)} %bitcast.121), channel_id=1, replica_groups=mesh['seq'=4,'ctx'=8,'head'=8] {'head'}, dimensions={0} | all-to-all | bytes 5898240 | tf_op jit(solution)/shard_map/all_to_all | solution.py:33
  285.2 2.4 reduce_sum.109
  287.6 0.9 copy.71
  288.5 14.1 %all-to-all-start.8 = ((bf16[360,32,16]{0,2,1:T(8,128)(2,1)}), bf16[360,32,16]{0,2,1:T(8,128)(2,1)S(1)}, u32[]{:S(2)}, u32[]{:S(2)}) async-start(bf16[360,32,16]{0,2,1:T(8,128)(2,1)} %bitcast.125), calls=%async_computation.8 | async-start | bytes 786432 | tf_op jit(solution)/shard_map/all_to_all | solution.py:159
  303.4 14.1 %all-to-all-done.8 = bf16[360,32,16]{0,2,1:T(8,128)(2,1)S(1)} async-done(((bf16[360,32,16]{0,2,1:T(8,128)(2,1)}), bf16[360,32,16]{0,2,1:T(8,128)(2,1)S(1)}, u32[]{:S(2)}, u32[]{:S(2)}) %all-to-all-start.8) | async-done | bytes 368672 | tf_op jit(solution)/shard_map/all_to_all | solution.py:159
  317.5 1.8 fusion.42
  (88 shorter events, 19.6 us)
Async XLA Ops:
  6.5 137.5 %copy-start = (bf16[512,2880]{0,1:T(8,128)(2,1)S(1)}, bf16[512,2880]{0,1:T(8,128)(2,1)}, u32[]{:S(2)}) copy-start(bf16[512,2880]{0,1:T(8,128)(2,1)} %param.21) | copy-start | bytes 8847364
  6.5 12.8 %copy-start.1 = (bf16[1,2048,1,64]{1,3,2,0:T(8,128)(2,1)S(1)}, bf16[1,2048,1,64]{1,3,2,0:T(8,128)(2,1)}, u32[]{:S(2)}) copy-start(bf16[1,2048,1,64]{1,3,2,0:T(8,128)(2,1)} %param.17) | copy-start | bytes 786436
  6.5 17.6 %copy-start.2 = (bf16[1,64,1,64]{3,1,2,0:T(8,128)(2,1)S(1)}, bf16[1,64,1,64]{3,1,2,0:T(8,128)(2,1)}, u32[]{:S(2)}) copy-start(bf16[1,64,1,64]{3,1,2,0:T(8,128)(2,1)} %param.19) | copy-start | bytes 24580
  6.5 17.6 %copy-start.3 = (bf16[1,64,1,64]{3,1,2,0:T(8,128)(2,1)S(1)}, bf16[1,64,1,64]{3,1,2,0:T(8,128)(2,1)}, u32[]{:S(2)}) copy-start(bf16[1,64,1,64]{3,1,2,0:T(8,128)(2,1)} %param.20) | copy-start | bytes 24580
  10.4 27.1 %all-to-all-start = ((bf16[8,1,1,512,64]{3,4,2,1,0:T(8,128)(2,1)}), bf16[8,1,1,512,64]{3,4,2,1,0:T(8,128)(2,1)}, u32[]{:S(2)}, u32[]{:S(2)}) async-start(bf16[8,1,1,512,64]{3,4,2,1,0:T(8,128)(2,1)} %broadcast_in_dim.65), calls=%async_computation | async-start | bytes 1048576 | tf_op jit(solution)/shard_map/all_to_all | solution.py:12
  37.4 77.7 %copy-start.7 = (s32[1,64,4]{1,2,0:T(4,128)S(1)}, s32[1,64,4]{1,2,0:T(4,128)}, u32[]{:S(2)}) copy-start(s32[1,64,4]{1,2,0:T(4,128)} %param.23) | copy-start | bytes 3076
  110.9 31.5 %all-to-all-start.1 = ((f32[8,1,512,64]{2,3,1,0:T(8,128)}), f32[8,1,512,64]{2,3,1,0:T(8,128)}, u32[]{:S(2)}, u32[]{:S(2)}) async-start(f32[8,1,512,64]{2,3,1,0:T(8,128)} %get-tuple-element.142), calls=%async_computation.1 | async-start | bytes 2097152 | tf_op jit(solution)/shard_map/all_to_all | solution.py:109
  116.9 0.6 copy-start.4
  144.1 9.2 %slice-start = ((s32[32,3]{0,1:T(4,128)}), s32[32,2]{0,1:T(2,128)S(1)}, s32[]{:S(2)}) async-start(s32[32,3]{0,1:T(4,128)} %copy-done.4), calls=%async_computation.10 | async-start | bytes 2048 | tf_op jit(solution)/shard_map/slice.1
  144.1 9.2 %copy-start.5 = (s32[256]{0:T(256)S(1)}, s32[256]{0:T(256)}, u32[]{:S(2)}) copy-start(s32[256]{0:T(256)} %eq.54) | copy-start | bytes 3076
  148.1 11.7 %all-to-all-start.4 = ((bf16[8,64,360]{2,1,0:T(8,128)(2,1)}), bf16[8,64,360]{2,1,0:T(8,128)(2,1)S(1)}, u32[]{:S(2)}, u32[]{:S(2)}) async-start(bf16[8,64,360]{2,1,0:T(8,128)(2,1)} %bitcast.105), calls=%async_computation.4 | async-start | bytes 786432 | tf_op jit(solution)/shard_map/all_to_all | solution.py:33
  161.6 8.2 %all-to-all-start.5 = ((f32[8,1,64]{2,1,0:T(1,128)}), f32[8,1,64]{2,1,0:T(1,128)S(1)}, u32[]{:S(2)}, u32[]{:S(2)}) async-start(f32[8,1,64]{2,1,0:T(1,128)} %broadcast_in_dim.69), calls=%async_computation.5 | async-start | bytes 8192 | tf_op jit(solution)/shard_map/all_to_all | solution.py:12
  164.9 70.6 %all-gather.2.cloned.1.call-start = ((), (), s32[]{:S(2)}) async-start(), calls=%async_computation.9 | async-start | bytes 3317760 | tf_op jit(solution)/shard_map/all_gather | solution.py:145
  285.2 17.4 %copy-start.6 = (f32[1,64,4]{1,2,0:T(4,128)S(1)}, f32[1,64,4]{1,2,0:T(4,128)}, u32[]{:S(2)}) copy-start(f32[1,64,4]{1,2,0:T(4,128)} %param.24) | copy-start | bytes 3076
  288.5 29.0 %all-to-all-start.8 = ((bf16[360,32,16]{0,2,1:T(8,128)(2,1)}), bf16[360,32,16]{0,2,1:T(8,128)(2,1)S(1)}, u32[]{:S(2)}, u32[]{:S(2)}) async-start(bf16[360,32,16]{0,2,1:T(8,128)(2,1)} %bitcast.125), calls=%async_computation.8 | async-start | bytes 786432 | tf_op jit(solution)/shard_map/all_to_all | solution.py:159
Sparse Core Ops, SparseCore 0:
  198.9 36.4 all-gather.1
where the time goes:
time: 328 us; the launch traced here: 326 us
  waiting for transfers between devices  96.7 us (29%)
  blocking collectives  79.1 us (24%)
  matrix products  56.1 us (17%)
  starting transfers between devices  35.8 us (11%)
  local copies, waits for them, and re-layouts  19 us (6%)
  other arithmetic  16 us (5%)
  between operations  13.6 us (4%)
  loops' own time  9.98 us (3%)
    all_to_all x1, blocking collectives, sent_and_summed(): lax.all_to_all(tiles, axis, split_axis=0, concat_axis=0, tiled=True)  37.1 us
    all_gather x1, waiting for transfers between devices, body(): piece = lax.all_gather(rows, 'head', axis=1, tiled=True)  36.6 us
    all_to_all x1, waiting for transfers between devices, body(): lax.all_to_all(pieces, 'ctx', split_axis=0, concat_axis=0, tiled=True)  24.6 us
    dot_general x8, matrix products, absorb(): jnp.einsum('hrd,hkd->hrk', block, keys, preferred_element_type=jnp.float32)  24 us
    all_to_all x1, blocking collectives, body(): lax.all_to_all(packed, ('seq', 'ctx'), split_axis=0, concat_axis=0, tiled...  23.9 us
    all_to_all x2, blocking collectives, body(): lax.all_to_all(pieces, 'ctx', split_axis=0, concat_axis=0, tiled=True)  18 us
    all_to_all x2, waiting for transfers between devices, sent_to_all(): return lax.all_to_all(copies, axis, split_axis=0, concat_axis=0, tiled=True)  15 us
    all_to_all x1, waiting for transfers between devices, body(): lax.all_to_all(expert_out, ('seq', 'ctx'), split_axis=1, concat_axis=1, t...  14.1 us
  transfers between devices with their start and end apart: 6, of which 6 were waited for; matrix products, arithmetic and copies ran while one was open for 3% of the time, Pallas kernels for 0%

commit v1 on v0

--- a/solution.py
+++ b/solution.py
@@ -142,7 +142,9 @@
     packed = packed.reshape(experts, CAP, normed.shape[1])
     arrived = lax.all_to_all(packed, ("seq", "ctx"), split_axis=0, concat_axis=0, tiled=True)
     rows = arrived.reshape(slots, normed.shape[1])
-    piece = lax.all_gather(rows, "head", axis=1, tiled=True)
+    piece = jnp.concatenate(
+        lax.all_to_all(jnp.stack([rows] * lax.axis_size("head")), "head", 0, 0), axis=1
+    )
     gate_rows = gate_weight[0]
     up_rows = up_weight[0]
     gate = jnp.dot(piece, gate_rows, preferred_element_type=jnp.float32)

time: 328 us -> 309 us (0.942)
  blocking collectives: 79.1 us -> 119 us
  waiting for transfers between devices: 96.7 us -> 59.3 us
  between operations: 13.6 us -> 0.24 us
  starting transfers between devices: 35.8 us -> 28.9 us
    all_to_all x0 -> x1, blocking collectives: none -> 38.2 us  [body(): lax.all_to_all(jnp.stack([rows] * lax.axis_size('head')), 'head', 0, 0)]
    all_gather x1 -> x0, waiting for transfers between devices: 36.6 us -> none  [body(): piece = lax.all_gather(rows, 'head', axis=1, tiled=True)]
    all_to_all x1, starting transfers between devices: 14.1 us -> 7.28 us  [body(): lax.all_to_all(expert_out, ('seq', 'ctx'), split_axis=1, concat_axis=1, t...]
  transfers between devices with their start and end apart: 6 -> 5, of which waited for: 6 -> 5; matrix products, arithmetic and copies ran while one was open for 3% -> 4% of each run, Pallas kernels for 0% -> 0%
where the time goes in v1:
time: 309 us; the launch traced here: 308 us
  blocking collectives  119 us (39%)
  waiting for transfers between devices  59.3 us (19%)
  matrix products  53.6 us (17%)
  starting transfers between devices  28.9 us (9%)
  local copies, waits for them, and re-layouts  20.8 us (7%)
  other arithmetic  16 us (5%)
  loops' own time  9.98 us (3%)
    all_to_all x1, blocking collectives, sent_and_summed(): lax.all_to_all(tiles, axis, split_axis=0, concat_axis=0, tiled=True)  38.8 us
    all_to_all x1, blocking collectives, body(): lax.all_to_all(jnp.stack([rows] * lax.axis_size('head')), 'head', 0, 0)  38.2 us
    all_to_all x1, blocking collectives, body(): lax.all_to_all(packed, ('seq', 'ctx'), split_axis=0, concat_axis=0, tiled...  24.1 us
    dot_general x8, matrix products, absorb(): jnp.einsum('hrd,hkd->hrk', block, keys, preferred_element_type=jnp.float32)  24 us
    all_to_all x1, waiting for transfers between devices, body(): lax.all_to_all(pieces, 'ctx', split_axis=0, concat_axis=0, tiled=True)  23.9 us
    all_to_all x2, blocking collectives, body(): lax.all_to_all(pieces, 'ctx', split_axis=0, concat_axis=0, tiled=True)  18 us
    all_to_all x2, waiting for transfers between devices, sent_to_all(): return lax.all_to_all(copies, axis, split_axis=0, concat_axis=0, tiled=True)  15 us
    all_to_all x1, waiting for transfers between devices, body(): lax.all_to_all(expert_out, ('seq', 'ctx'), split_axis=1, concat_axis=1, t...  14.1 us
  transfers between devices with their start and end apart: 5, of which 5 were waited for; matrix products, arithmetic and copies ran while one was open for 4% of the time, Pallas kernels for 0%

profile of v1, /device:TPU:1, one launch (start us, length us, event | category | flops | bytes accessed | tf_op | source)
XLA Modules:
  0.0 307.9 jit_solution(2329043552672069988)
XLA Ops:
  0.0 2.7 convolution_convert_fusion.3
  3.8 9.0 %all-to-all-start = ((bf16[8,1,1,512,64]{3,4,2,1,0:T(8,128)(2,1)}), bf16[8,1,1,512,64]{3,4,2,1,0:T(8,128)(2,1)}, u32[]{:S(2)}, u32[]{:S(2)}) async-start(bf16[8,1,1,512,64]{3,4,2,1,0:T(8,128)(2,1)} %broadcast_in_dim.65), calls=%async_computation | async-start | bytes 1048576 | tf_op jit(solution)/shard_map/all_to_all | solution.py:12
  12.9 1.0 copy.59
  13.9 1.9 copy.60
  17.6 2.2 maximum_bitcast_fusion
  19.8 11.1 %all-to-all-done = bf16[8,1,1,512,64]{3,4,2,1,0:T(8,128)(2,1)} async-done(((bf16[8,1,1,512,64]{3,4,2,1,0:T(8,128)(2,1)}), bf16[8,1,1,512,64]{3,4,2,1,0:T(8,128)(2,1)}, u32[]{:S(2)}, u32[]{:S(2)}) %all-to-all-start) | async-done | bytes 524320 | tf_op jit(solution)/shard_map/all_to_all | solution.py:12
  30.9 55.5 %while.17 = (s32[]{:T(128)}, f32[8,1,512]{2,1,0:T(1,128)S(1)}, f32[8,1,512]{2,1,0:T(1,128)S(1)}, f32[8,1,512,64]{2,3,1,0:T(8,128)}, s32[8]{0:T(128)S(1)}, /*inde...) while((s32[]{:T(128)}, f32[8,1,512]{2,1,0:T(1,128)S(1)}, ...), condition=%wide.region_3.4_spmd.clone, body=%wide.region_0.3_spmd.clone.sunk | while | flops 290915840 | bytes 14024361 | solution.py:108
  32.7 3.0 fusion.82
  35.8 1.4 fusion.84
  39.7 3.0 fusion.82
  42.7 1.4 fusion.84
  46.6 3.0 fusion.82
  49.6 1.4 fusion.84
  53.5 3.0 fusion.82
  56.6 1.4 fusion.84
  60.5 3.0 fusion.82
  63.5 1.4 fusion.84
  67.4 3.0 fusion.82
  70.4 1.4 fusion.84
  74.3 3.0 fusion.82
  77.4 1.4 fusion.84
  81.3 3.0 fusion.82
  84.3 1.4 fusion.84
  86.4 9.0 %all_to_all.58 = f32[8,1,512]{2,1,0:T(1,128)S(1)} all-to-all(f32[8,1,512]{2,1,0:T(1,128)S(1)} %get-tuple-element.143), channel_id=1, replica_groups=mesh['seq'=4,'ctx'=8,'head'=8] {'ctx'}, dimensions={0} | all-to-all | bytes 32768 | tf_op jit(solution)/shard_map/all_to_all | solution.py:109
  95.4 9.0 %all_to_all.59 = f32[8,1,512]{2,1,0:T(1,128)S(1)} all-to-all(f32[8,1,512]{2,1,0:T(1,128)S(1)} %get-tuple-element.144), channel_id=1, replica_groups=mesh['seq'=4,'ctx'=8,'head'=8] {'ctx'}, dimensions={0} | all-to-all | bytes 32768 | tf_op jit(solution)/shard_map/all_to_all | solution.py:109
  104.3 4.2 %all-to-all-start.1 = ((f32[8,1,512,64]{2,3,1,0:T(8,128)}), f32[8,1,512,64]{2,3,1,0:T(8,128)}, u32[]{:S(2)}, u32[]{:S(2)}) async-start(f32[8,1,512,64]{2,3,1,0:T(8,128)} %get-tuple-element.142), calls=%async_computation.1 | async-start | bytes 2097152 | tf_op jit(solution)/shard_map/all_to_all | solution.py:109
  111.9 23.9 %all-to-all-done.1 = f32[8,1,512,64]{2,3,1,0:T(8,128)} async-done(((f32[8,1,512,64]{2,3,1,0:T(8,128)}), f32[8,1,512,64]{2,3,1,0:T(8,128)}, u32[]{:S(2)}, u32[]{:S(2)}) %all-to-all-start.1) | async-done | bytes 1048608 | tf_op jit(solution)/shard_map/all_to_all | solution.py:109
  135.8 1.4 multiply_reduce_fusion
  137.4 1.7 convolution_convert_fusion.1
  139.1 1.5 reshape.195
  141.5 5.1 %all-to-all-start.4 = ((bf16[8,64,360]{2,1,0:T(8,128)(2,1)}), bf16[8,64,360]{2,1,0:T(8,128)(2,1)S(1)}, u32[]{:S(2)}, u32[]{:S(2)}) async-start(bf16[8,64,360]{2,1,0:T(8,128)(2,1)} %bitcast.108), calls=%async_computation.4 | async-start | bytes 786432 | tf_op jit(solution)/shard_map/all_to_all | solution.py:33
  146.9 6.3 %all-to-all-done.4 = bf16[8,64,360]{2,1,0:T(8,128)(2,1)S(1)} async-done(((bf16[8,64,360]{2,1,0:T(8,128)(2,1)}), bf16[8,64,360]{2,1,0:T(8,128)(2,1)S(1)}, u32[]{:S(2)}, u32[]{:S(2)}) %all-to-all-start.4) | async-done | bytes 368672 | tf_op jit(solution)/shard_map/all_to_all | solution.py:33
  153.2 1.0 multiply_reduce_fusion.1
  154.9 3.3 %all-to-all-start.5 = ((f32[8,1,64]{2,1,0:T(1,128)}), f32[8,1,64]{2,1,0:T(1,128)S(1)}, u32[]{:S(2)}, u32[]{:S(2)}) async-start(f32[8,1,64]{2,1,0:T(1,128)} %broadcast_in_dim.69), calls=%async_computation.5 | async-start | bytes 8192 | tf_op jit(solution)/shard_map/all_to_all | solution.py:12
  159.1 4.0 %all-to-all-done.5 = f32[8,1,64]{2,1,0:T(1,128)S(1)} async-done(((f32[8,1,64]{2,1,0:T(1,128)}), f32[8,1,64]{2,1,0:T(1,128)S(1)}, u32[]{:S(2)}, u32[]{:S(2)}) %all-to-all-start.5) | async-done | bytes 2080 | tf_op jit(solution)/shard_map/all_to_all | solution.py:12
  163.1 2.0 convolution_convert_fusion.2
  165.1 1.2 copy.71
  166.3 24.1 %all_to_all.60 = bf16[32,16,360]{2,1,0:T(8,128)(2,1)} all-to-all(bf16[32,16,360]{2,1,0:T(8,128)(2,1)S(1)} %bitcast.131), channel_id=1, replica_groups=mesh['seq'=4,'ctx'=8,'head'=8] {'seq','ctx'}, dimensions={0} | all-to-all | bytes 737280 | tf_op jit(solution)/shard_map/all_to_all | solution.py:143
  190.4 1.2 copy.72
  191.7 38.2 %all_to_all.61 = bf16[8,512,360]{1,2,0:T(8,128)(2,1)S(1)} all-to-all(bf16[8,512,360]{1,2,0:T(8,128)(2,1)S(1)} %stack.3), channel_id=1, replica_groups=mesh['seq'=4,'ctx'=8,'head'=8] {'head'}, dimensions={0} | all-to-all | bytes 5898240 | tf_op jit(solution)/shard_map/all_to_all | solution.py:146
  230.0 1.6 copy-done.1
  231.6 2.2 fusion.30
  233.8 7.9 %convolution_convert_fusion = bf16[512,2880]{0,1:T(8,128)(2,1)} fusion(bf16[1,360,2880]{2,1,0:T(8,128)(2,1)} %param.27, bf16[512,2880]{0,1:T(8,128)(2,1)} %bitcast.125, bf16[1,2880,360]{1,2,0:T(8,128)(2,1)} %param.26, f32[512,360]{0,1:T(8,128)} %fusion.30), kind=kOutput, calls=%fused_computation.25 | convolution fusion | flops 2126315520 | bytes 10782720 | tf_op jit(solution)/shard_map/fd,rf->dr/dot_general | solution.py:155
  241.7 38.8 %all_to_all.62 = bf16[8,360,512]{2,1,0:T(8,128)(2,1)} all-to-all(bf16[8,360,512]{2,1,0:T(8,128)(2,1)} %bitcast.126), channel_id=1, replica_groups=mesh['seq'=4,'ctx'=8,'head'=8] {'head'}, dimensions={0} | all-to-all | bytes 5898240 | tf_op jit(solution)/shard_map/all_to_all | solution.py:33
  280.5 2.4 reduce_sum.109
  283.8 7.3 %all-to-all-start.9 = ((bf16[360,32,16]{0,2,1:T(8,128)(2,1)}), bf16[360,32,16]{0,2,1:T(8,128)(2,1)S(1)}, u32[]{:S(2)}, u32[]{:S(2)}) async-start(bf16[360,32,16]{0,2,1:T(8,128)(2,1)} %bitcast.130), calls=%async_computation.9 | async-start | bytes 786432 | tf_op jit(solution)/shard_map/all_to_all | solution.py:161
  291.9 14.1 %all-to-all-done.9 = bf16[360,32,16]{0,2,1:T(8,128)(2,1)S(1)} async-done(((bf16[360,32,16]{0,2,1:T(8,128)(2,1)}), bf16[360,32,16]{0,2,1:T(8,128)(2,1)S(1)}, u32[]{:S(2)}, u32[]{:S(2)}) %all-to-all-start.9) | async-done | bytes 368672 | tf_op jit(solution)/shard_map/all_to_all | solution.py:161
  306.0 1.8 fusion.42
  (89 shorter events, 21.3 us)
Async XLA Ops:
  0.0 137.4 %copy-start = (bf16[512,2880]{0,1:T(8,128)(2,1)S(1)}, bf16[512,2880]{0,1:T(8,128)(2,1)}, u32[]{:S(2)}) copy-start(bf16[512,2880]{0,1:T(8,128)(2,1)} %param.21) | copy-start | bytes 8847364
  0.0 12.9 %copy-start.2 = (bf16[1,2048,1,64]{1,3,2,0:T(8,128)(2,1)S(1)}, bf16[1,2048,1,64]{1,3,2,0:T(8,128)(2,1)}, u32[]{:S(2)}) copy-start(bf16[1,2048,1,64]{1,3,2,0:T(8,128)(2,1)} %param.17) | copy-start | bytes 786436
  0.0 17.6 %copy-start.3 = (bf16[1,64,1,64]{3,1,2,0:T(8,128)(2,1)S(1)}, bf16[1,64,1,64]{3,1,2,0:T(8,128)(2,1)}, u32[]{:S(2)}) copy-start(bf16[1,64,1,64]{3,1,2,0:T(8,128)(2,1)} %param.19) | copy-start | bytes 24580
  0.0 17.6 %copy-start.4 = (bf16[1,64,1,64]{3,1,2,0:T(8,128)(2,1)S(1)}, bf16[1,64,1,64]{3,1,2,0:T(8,128)(2,1)}, u32[]{:S(2)}) copy-start(bf16[1,64,1,64]{3,1,2,0:T(8,128)(2,1)} %param.20) | copy-start | bytes 24580
  3.8 27.1 %all-to-all-start = ((bf16[8,1,1,512,64]{3,4,2,1,0:T(8,128)(2,1)}), bf16[8,1,1,512,64]{3,4,2,1,0:T(8,128)(2,1)}, u32[]{:S(2)}, u32[]{:S(2)}) async-start(bf16[8,1,1,512,64]{3,4,2,1,0:T(8,128)(2,1)} %broadcast_in_dim.65), calls=%async_computation | async-start | bytes 1048576 | tf_op jit(solution)/shard_map/all_to_all | solution.py:12
  104.3 31.4 %all-to-all-start.1 = ((f32[8,1,512,64]{2,3,1,0:T(8,128)}), f32[8,1,512,64]{2,3,1,0:T(8,128)}, u32[]{:S(2)}, u32[]{:S(2)}) async-start(f32[8,1,512,64]{2,3,1,0:T(8,128)} %get-tuple-element.142), calls=%async_computation.1 | async-start | bytes 2097152 | tf_op jit(solution)/shard_map/all_to_all | solution.py:109
  111.0 0.6 copy-start.5
  137.4 9.2 %slice-start = ((s32[32,3]{0,1:T(4,128)}), s32[32,2]{0,1:T(2,128)S(1)}, s32[]{:S(2)}) async-start(s32[32,3]{0,1:T(4,128)} %copy-done.5), calls=%async_computation.10 | async-start | bytes 2048 | tf_op jit(solution)/shard_map/slice.1
  137.4 9.2 %copy-start.6 = (s32[256]{0:T(256)S(1)}, s32[256]{0:T(256)}, u32[]{:S(2)}) copy-start(s32[256]{0:T(256)} %eq.54) | copy-start | bytes 3076
  141.5 11.7 %all-to-all-start.4 = ((bf16[8,64,360]{2,1,0:T(8,128)(2,1)}), bf16[8,64,360]{2,1,0:T(8,128)(2,1)S(1)}, u32[]{:S(2)}, u32[]{:S(2)}) async-start(bf16[8,64,360]{2,1,0:T(8,128)(2,1)} %bitcast.108), calls=%async_computation.4 | async-start | bytes 786432 | tf_op jit(solution)/shard_map/all_to_all | solution.py:33
  154.9 8.2 %all-to-all-start.5 = ((f32[8,1,64]{2,1,0:T(1,128)}), f32[8,1,64]{2,1,0:T(1,128)S(1)}, u32[]{:S(2)}, u32[]{:S(2)}) async-start(f32[8,1,64]{2,1,0:T(1,128)} %broadcast_in_dim.69), calls=%async_computation.5 | async-start | bytes 8192 | tf_op jit(solution)/shard_map/all_to_all | solution.py:12
  191.7 39.9 %copy-start.8 = (bf16[1,2880,360]{1,2,0:T(8,128)(2,1)S(1)}, bf16[1,2880,360]{1,2,0:T(8,128)(2,1)}, u32[]{:S(2)}) copy-start(bf16[1,2880,360]{1,2,0:T(8,128)(2,1)} %param.25) | copy-start | bytes 6220804
  230.0 1.6 copy-start.1
  280.5 10.6 %copy-start.7 = (f32[1,64,4]{1,2,0:T(4,128)S(1)}, f32[1,64,4]{1,2,0:T(4,128)}, u32[]{:S(2)}) copy-start(f32[1,64,4]{1,2,0:T(4,128)} %param.24) | copy-start | bytes 3076
  283.8 22.2 %all-to-all-start.9 = ((bf16[360,32,16]{0,2,1:T(8,128)(2,1)}), bf16[360,32,16]{0,2,1:T(8,128)(2,1)S(1)}, u32[]{:S(2)}, u32[]{:S(2)}) async-start(bf16[360,32,16]{0,2,1:T(8,128)(2,1)} %bitcast.130), calls=%async_computation.9 | async-start | bytes 786432 | tf_op jit(solution)/shard_map/all_to_all | solution.py:161
